TPU v7x, 32 devices: a whole 2x2x4 slice. The times are simulated.
32 devices in a mesh: gx: 8 (over z, x), gy: 4 (over y, core).
Axes of the slice: x: 2, y: 2, z: 4, core: 2. Of those that a mesh axis runs over, the one named last changes fastest.
Arguments:
- tokens: bfloat16 [256, 8192], P(None, 'gx'), may hold values from -16 to 16
- attn_gain: bfloat16 [8192], P('gx'), may hold values from 0.25 to 1.75
- qkv_weight: bfloat16 [8192, 10240], P('gx', 'gy'), may hold values from -0.0625 to 0.0625
- cache_keys: bfloat16 [256, 8, 512, 128], P('gx', 'gy'), may hold values from -160 to 160
- cache_values: bfloat16 [256, 8, 512, 128], P('gx', 'gy'), may hold values from -6 to 6
- lengths: int32 [256], replicated, may hold values from 1 to 512
- live_mask: int32 [256], replicated, may hold values 0 or 1
- out_weight: bfloat16 [8192, 8192], P('gy', 'gx'), may hold values from -0.0625 to 0.0625
- mlp_gain: bfloat16 [8192], P('gx'), may hold values from 0.25 to 1.75
- gate_weight: bfloat16 [8192, 28672], P('gx', 'gy'), may hold values from -0.0625 to 0.0625
- up_weight: bfloat16 [8192, 28672], P('gx', 'gy'), may hold values from -0.0625 to 0.0625
- down_weight: bfloat16 [28672, 8192], P('gy', 'gx'), may hold values from -0.03125 to 0.03125
Outputs:
- updated: bfloat16 [256, 8192], P('gy', 'gx')
All inputs are finite; a program needn't handle non-finite values.
Results may differ from a plain program's by a relative error of at most 0.0095.
Values may be sent and summed in bfloat16 or wider, within the bound.
A program may use at most 128 MiB of HBM per device.

v0:
```python
import jax
import jax.numpy as jnp
from jax import lax
from jax.sharding import PartitionSpec as P

D = 8192
H = 64
KVH = 8
HD = 128


ROPE_BASE = 500000.0
NORM_EPS = 1e-05
MASKED = -1e30


def rotate_pairs(vectors, positions):
    half_width = vectors.shape[-1] // 2
    index_float = jnp.arange(half_width).astype(jnp.float32)
    inv_freq = jnp.exp(index_float * (-2.0 * jnp.log(ROPE_BASE) / vectors.shape[-1]))
    angles = positions.astype(jnp.float32)[:, None] * inv_freq[None, :]
    cosine = jnp.cos(angles)[:, None, :]
    sine_part = jnp.sin(angles)[:, None, :]
    low_half = vectors[..., :half_width]
    high_half = vectors[..., half_width:]
    return jnp.concatenate(
        (low_half * cosine - high_half * sine_part, high_half * cosine + low_half * sine_part),
        axis=-1,
    )


def make_heads(projected, square_rows, positions, groups, per_kv):
    row_count = projected.shape[0]
    attn_scale = lax.rsqrt(square_rows / D + NORM_EPS)
    shaped = (projected * attn_scale[:, None]).reshape(row_count, groups, per_kv + 2, HD)
    query_rows = rotate_pairs(
        shaped[:, :, :per_kv].reshape(row_count, groups * per_kv, HD), positions
    )
    query_rows = query_rows.astype(jnp.bfloat16).reshape(row_count, groups, per_kv, HD)
    fresh_key_rows = rotate_pairs(shaped[:, :, per_kv], positions).astype(jnp.bfloat16)
    new_values = shaped[:, :, per_kv + 1].astype(jnp.bfloat16)
    return (query_rows, fresh_key_rows, new_values)


def attend(query_rows, fresh_key_rows, new_values, cache_keys, cache_values, lengths):
    score_scale = query_rows.shape[-1] ** (-0.5)
    stored_entries = (
        jnp.einsum("bgqd,bgld->bgql", query_rows, cache_keys, preferred_element_type=jnp.float32)
        * score_scale
    )
    places = jnp.arange(cache_keys.shape[2])
    valid = places[None, None, None, :] < lengths[:, None, None, None]
    stored_entries = jnp.where(valid, stored_entries, MASKED)
    self_token = (
        jnp.einsum("bgqd,bgd->bgq", query_rows, fresh_key_rows, preferred_element_type=jnp.float32)
        * score_scale
    )
    peak = jnp.maximum(jnp.max(stored_entries, axis=-1), self_token)
    attention_probs = jnp.where(valid, jnp.exp(stored_entries - peak[..., None]), 0.0).astype(
        jnp.bfloat16
    )
    weight_sum = jnp.sum(attention_probs.astype(jnp.float32), axis=-1)
    blended_values = jnp.einsum(
        "bgql,bgld->bgqd", attention_probs, cache_values, preferred_element_type=jnp.float32
    )
    own_weight = jnp.exp(self_token - peak).astype(jnp.bfloat16).astype(jnp.float32)
    totals = weight_sum + own_weight
    blended_values = (
        blended_values + own_weight[..., None] * new_values.astype(jnp.float32)[:, :, None, :]
    )
    return (blended_values / totals[..., None]).astype(jnp.bfloat16)


def per_device(
    tokens,
    attn_gain,
    qkv_weight,
    cache_keys,
    cache_values,
    lengths,
    live_mask,
    out_weight,
    mlp_gain,
    gate_weight,
    up_weight,
    down_weight,
):
    batch_size = tokens.shape[0]
    local_rows = batch_size // lax.axis_size("gx")
    groups = cache_keys.shape[1]
    per_kv = H // KVH
    row_start = lax.axis_index("gx") * local_rows
    wide_in = tokens.astype(jnp.float32)
    scaled = (wide_in * attn_gain.astype(jnp.float32)).astype(jnp.bfloat16)
    squares = jnp.sum(wide_in * wide_in, axis=1)
    partial_sum = jnp.dot(scaled, qkv_weight, preferred_element_type=jnp.float32)
    own_proj, own_squares = (
        lax.psum_scatter(partial_sum, "gx", scatter_dimension=0, tiled=True),
        lax.psum_scatter(squares, "gx", scatter_dimension=0, tiled=True),
    )
    own_lengths = lax.dynamic_slice_in_dim(lengths, row_start, local_rows, 0)
    query_rows, fresh_key_rows, new_values = make_heads(
        own_proj, own_squares, own_lengths, groups, per_kv
    )
    attn = attend(query_rows, fresh_key_rows, new_values, cache_keys, cache_values, own_lengths)
    attn = attn.reshape(local_rows, groups * per_kv * HD)
    proj_part = jnp.dot(
        lax.all_gather(attn, "gx", axis=0, tiled=True),
        out_weight,
        preferred_element_type=jnp.float32,
    )
    attn_proj = lax.psum(proj_part, "gy")
    alive_col = live_mask.astype(jnp.float32)[:, None]
    residual = (wide_in + alive_col * attn_proj).astype(jnp.bfloat16)
    resid_wide = residual.astype(jnp.float32)
    mlp_in = (resid_wide * mlp_gain.astype(jnp.float32)).astype(jnp.bfloat16)
    resid_squares = jnp.sum(resid_wide * resid_wide, axis=1)
    out_rows = batch_size // lax.axis_size("gy")
    out_start = lax.axis_index("gy") * out_rows
    square_all = lax.psum(resid_squares, "gx")
    hidden_width = gate_weight.shape[1]
    stacked = lax.psum_scatter(
        jnp.concatenate(
            (
                jnp.dot(mlp_in, gate_weight, preferred_element_type=jnp.float32),
                jnp.dot(mlp_in, up_weight, preferred_element_type=jnp.float32),
            ),
            axis=1,
        ),
        "gx",
        scatter_dimension=0,
        tiled=True,
    )
    own_all = lax.dynamic_slice_in_dim(square_all, row_start, local_rows, 0)
    mlp_scale = lax.rsqrt(own_all / D + NORM_EPS)[:, None]
    hidden_share = (
        jax.nn.silu(stacked[:, :hidden_width] * mlp_scale) * (stacked[:, hidden_width:] * mlp_scale)
    ).astype(jnp.bfloat16)
    down_full = jnp.dot(
        lax.all_gather(hidden_share, "gx", axis=0, tiled=True),
        down_weight,
        preferred_element_type=jnp.float32,
    )
    down_sum = lax.psum_scatter(down_full, "gy", scatter_dimension=0, tiled=True)
    resid_rows = lax.dynamic_slice_in_dim(resid_wide, out_start, out_rows, 0)
    alive_rows = lax.dynamic_slice_in_dim(alive_col, out_start, out_rows, 0)
    return (resid_rows + alive_rows * down_sum).astype(jnp.bfloat16)


def solution(mesh):
    return jax.shard_map(
        per_device,
        mesh=mesh,
        in_specs=(
            P(None, "gx"),
            P("gx"),
            P("gx", "gy"),
            P("gx", "gy", None, None),
            P("gx", "gy", None, None),
            P(),
            P(),
            P("gy", "gx"),
            P("gx"),
            P("gx", "gy"),
            P("gx", "gy"),
            P("gy", "gx"),
        ),
        out_specs=P("gy", "gx"),
        check_vma=False,
    )
```

profile of v0, /device:TPU:0, one launch (start us, length us, event | category | flops | bytes accessed | tf_op | source)
XLA Modules:
  0.0 550.8 jit_solution(7446192917062346969)
XLA Ops:
  6.5 0.7 convert_element_type.66
  7.2 5.7 %fusion.9 = f32[256,2560]{1,0:T(8,128)} fusion(bf16[1024,2560]{1,0:T(8,128)(2,1)} %param.14, bf16[256,1024]{1,0:T(8,128)(2,1)} %param.12, f32[1024]{0:T(1024)S(1)} %convert_element_type.66), kind=kOutput, calls=%fused_computation.21 | convolution fusion | flops 1342963712 | bytes 8392704 | tf_op jit(solution)/shard_map/dot_general | solution.py:96
  13.1 0.6 dynamic-slice.4
  14.5 23.5 %all-reduce = f32[256]{0:T(256)S(1)} all-reduce(f32[256]{0:T(256)S(1)} %fusion.4), channel_id=3, replica_groups=mesh['gx'=8,'gy'=4] {'gx'}, use_global_device_ids=true, to_apply=%region_2.0.clone | all-reduce | flops 256 | bytes 2048
  38.4 48.8 %reduce-scatter.4.cloned.1.call-done = f32[32,2560]{1,0:T(8,128)} async-done(((f32[256,2560]{1,0:T(8,128)}), f32[32,2560]{1,0:T(8,128)}) %reduce-scatter.4.cloned.1.call-update) | async-done | bytes 327696 | tf_op jit(solution)/shard_map/reduce_scatter | solution.py:98
  87.1 1.1 broadcast_multiply_fusion
  89.0 5.8 %fusion.29 = (f32[32,2,8]{2,1,0:T(2,128)S(1)}, f32[32,2,8,512]{3,2,1,0:T(8,128)S(1)}) fusion(bf16[32,2,512,128]{3,2,1,0:T(8,128)(2,1)} %param.15, bf16[32,2,8,64]{3,2,1,0:T(8,128)(2,1)S(1)} %get-tuple-element.12, bf16[32,2,8,64]{3,2,1,0:T(8,128)(2,1)S(1)} %get-tuple-element.11, pred[32,512]{1,0:T(8,128)(4,1)S(1)} %iota_compare_fusion), kind=kOutput, calls=%fused_computation.57 | convolution fusion | flops 68156928 | bytes 9586688 | tf_op jit(solution)/shard_map/bgqd,bgld->bgql/dot_general | solution.py:48
  94.9 0.4 convert_reduce_fusion
  95.4 4.7 fusion.2
  100.1 0.7 copy.19
  100.8 39.5 %all-gather.3.cloned.1.call-done = bf16[256,2048]{1,0:T(8,128)(2,1)} async-done(((bf16[32,2048]{1,0:T(8,128)(2,1)}), bf16[256,2048]{1,0:T(8,128)(2,1)}) %all-gather.3.cloned.1.call-update) | async-done | bytes 1048592 | tf_op jit(solution)/shard_map/all_gather | solution.py:108
  140.4 4.7 fusion.30
  145.3 35.1 %all-reduce.3.cloned.1.call-done = f32[256,1024]{1,0:T(8,128)} async-done(((f32[256,1024]{1,0:T(8,128)}), f32[256,1024]{1,0:T(8,128)}) %all-reduce.3.cloned.1.call-update) | async-done | bytes 1048592 | tf_op jit(solution)/shard_map/psum | solution.py:112
  180.3 1.5 multiply_reduce_fusion
  181.9 7.3 %fusion.12 = f32[256,7168]{1,0:T(8,128)S(1)} fusion(bf16[1024,7168]{1,0:T(8,128)(2,1)} %param.22, f32[256,1024]{1,0:T(8,128)S(1)} %get-tuple-element.6, f32[1024]{0:T(1024)S(1)} %convert_element_type.77), kind=kOutput, calls=%fused_computation.27 | convolution fusion | flops 3758620672 | bytes 23072768 | tf_op jit(solution)/shard_map/dot_general | solution.py:126
  189.2 7.3 %fusion.13 = f32[256,7168]{1,0:T(8,128)S(1)} fusion(bf16[1024,7168]{1,0:T(8,128)(2,1)} %param.21, f32[256,1024]{1,0:T(8,128)S(1)} %get-tuple-element.6, f32[1024]{0:T(1024)S(1)} %convert_element_type.77), kind=kOutput, calls=%fused_computation.28 | convolution fusion | flops 3758620672 | bytes 23072768 | tf_op jit(solution)/shard_map/dot_general | solution.py:125
  196.4 5.5 pad_maximum_fusion
  202.0 22.0 %psum.15 = f32[256]{0:T(256)S(1)} all-reduce(f32[256]{0:T(256)S(1)} %get-tuple-element.5), channel_id=1, replica_groups=mesh['gx'=8,'gy'=4] {'gx'}, use_global_device_ids=true, to_apply=%region_8.9 | all-reduce | flops 256 | bytes 2048 | tf_op jit(solution)/shard_map/psum | solution.py:120
  224.1 215.3 %reduce-scatter.6.cloned.1.call-done = f32[32,14336]{1,0:T(8,128)} async-done(((f32[256,14336]{1,0:T(8,128)}), f32[32,14336]{1,0:T(8,128)}) %reduce-scatter.6.cloned.1.call-update) | async-done | bytes 1835024 | tf_op jit(solution)/shard_map/reduce_scatter | solution.py:122
  439.4 2.6 fusion.7
  442.2 65.2 %all-gather.5.cloned.1.call-done = bf16[256,7168]{1,0:T(8,128)(2,1)} async-done(((bf16[32,7168]{1,0:T(8,128)(2,1)}), bf16[256,7168]{1,0:T(8,128)(2,1)}) %all-gather.5.cloned.1.call-update) | async-done | bytes 3670032 | tf_op jit(solution)/shard_map/all_gather | solution.py:140
  507.4 11.2 %fusion.31 = f32[256,1024]{1,0:T(8,128)} fusion(bf16[256,7168]{1,0:T(8,128)(2,1)} %all-gather.5.cloned.1.call-done, bf16[7168,1024]{1,0:T(8,128)(2,1)} %param.23), kind=kOutput, calls=%fused_computation.59 | convolution fusion | flops 3758096384 | bytes 19398656 | tf_op jit(solution)/shard_map/dot_general | solution.py:139
  518.7 23.6 %reduce-scatter.8.cloned.1.call-done = f32[64,1024]{1,0:T(8,128)} async-done(((f32[256,1024]{1,0:T(8,128)}), f32[64,1024]{1,0:T(8,128)}) %reduce-scatter.8.cloned.1.call-update) | async-done | bytes 262160 | tf_op jit(solution)/shard_map/reduce_scatter | solution.py:144
  542.3 1.7 add_convert_fusion
  (42 shorter events, 2.1 us)
Async XLA Ops:
  6.5 80.6 %reduce-scatter.4.cloned.1.call-start = ((), (), s32[]{:S(2)}) async-start(), calls=%async_computation.3 | async-start | bytes 2949120 | tf_op jit(solution)/shard_map/reduce_scatter | solution.py:98
  7.2 5.8 %copy-start.4 = (u32[32]{0:T(128)S(1)}, u32[32]{0:T(128)}, u32[]{:S(2)}) copy-start(u32[32]{0:T(128)} %constant.41) | copy-start | bytes 388
  7.2 7.1 %copy-start = (bf16[256,1024]{1,0:T(8,128)(2,1)S(1)}, bf16[256,1024]{1,0:T(8,128)(2,1)}, u32[]{:S(2)}) copy-start(bf16[256,1024]{1,0:T(8,128)(2,1)} %param.12) | copy-start | bytes 1572868
  7.2 30.8 %copy-start.3 = (s32[256]{0:T(256)S(1)}, s32[256]{0:T(256)}, u32[]{:S(2)}) copy-start(s32[256]{0:T(256)} %param.17) | copy-start | bytes 3076
  13.0 127.4 %all-gather.3.cloned.1.call-start = ((), (), s32[]{:S(2)}) async-start(), calls=%async_computation.4 | async-start | bytes 1179648 | tf_op jit(solution)/shard_map/all_gather | solution.py:108
  95.3 49.9 %copy-start.2 = (s32[256]{0:T(256)S(1)}, s32[256]{0:T(256)}, u32[]{:S(2)}) copy-start(s32[256]{0:T(256)} %param.18) | copy-start | bytes 3076
  95.3 49.9 %copy-start.1 = (bf16[1024]{0:T(1024)(128)(2,1)S(1)}, bf16[1024]{0:T(1024)(128)(2,1)}, u32[]{:S(2)}) copy-start(bf16[1024]{0:T(1024)(128)(2,1)} %param.20) | copy-start | bytes 6148
  100.8 79.5 %all-reduce.3.cloned.1.call-start = ((), (), s32[]{:S(2)}) async-start(), calls=%async_computation.5 | async-start | bytes 2097152 | tf_op jit(solution)/shard_map/psum | solution.py:112
  145.2 294.2 %reduce-scatter.6.cloned.1.call-start = ((), (), s32[]{:S(2)}) async-start(), calls=%async_computation.6 | async-start | bytes 16515072 | tf_op jit(solution)/shard_map/reduce_scatter | solution.py:122
  201.9 305.5 %all-gather.5.cloned.1.call-start = ((), (), s32[]{:S(2)}) async-start(), calls=%async_computation.7 | async-start | bytes 4128768 | tf_op jit(solution)/shard_map/all_gather | solution.py:140
  442.0 100.4 %reduce-scatter.8.cloned.1.call-start = ((), (), s32[]{:S(2)}) async-start(), calls=%async_computation.8 | async-start | bytes 1310720 | tf_op jit(solution)/shard_map/reduce_scatter | solution.py:144
Sparse Core Ops, SparseCore 0:
  13.1 73.9 reduce-scatter.3
  100.9 39.4 all-gather.2
  145.3 35.0 all-reduce.2
  202.1 237.2 reduce-scatter.5
  442.1 65.2 all-gather.4
  518.8 23.4 reduce-scatter.7
where the time goes:
time: 551 us
  waiting for transfers between devices  428 us (78%)
  matrix products  47 us (9%)
  blocking collectives  45.5 us (8%)
  other arithmetic  14.6 us (3%)
  between operations  14.3 us (3%)
    reduce_scatter x1, waiting for transfers between devices, per_device(): lax.psum_scatter(jnp.concatenate((jnp.dot(mlp_in, gate_weight, preferred_...  215 us
    all_gather x1, waiting for transfers between devices, per_device(): lax.all_gather(hidden_share, 'gx', axis=0, tiled=True)  65.2 us
    reduce_scatter x1, waiting for transfers between devices, per_device(): lax.psum_scatter(partial_sum, 'gx', scatter_dimension=0, tiled=True)  48.8 us
    all_gather x1, waiting for transfers between devices, per_device(): lax.all_gather(attn, 'gx', axis=0, tiled=True)  39.5 us
    psum x1, waiting for transfers between devices, per_device(): attn_proj = lax.psum(proj_part, 'gy')  35.1 us
    reduce_scatter x1, waiting for transfers between devices, per_device(): lax.psum_scatter(down_full, 'gy', scatter_dimension=0, tiled=True)  23.6 us
    unnamed x1, blocking collectives  23.5 us
    psum x1, blocking collectives, per_device(): square_all = lax.psum(resid_squares, 'gx')  22 us
  transfers between devices with their start and end apart: 6, of which 6 were waited for; matrix products, arithmetic and copies ran while one was open for 0% of the time, Pallas kernels for 0%

commit v1 on v0

--- a/solution.py
+++ b/solution.py
@@ -1,6 +1,10 @@
+import functools
+
 import jax
 import jax.numpy as jnp
 from jax import lax
+from jax.experimental import pallas as pl
+from jax.experimental.pallas import tpu as pltpu
 from jax.sharding import PartitionSpec as P
 
 D = 8192
@@ -69,6 +73,198 @@
         blended_values + own_weight[..., None] * new_values.astype(jnp.float32)[:, :, None, :]
     )
     return (blended_values / totals[..., None]).astype(jnp.bfloat16)
+
+
+def greet(axis, n, me):
+    barrier = pltpu.get_barrier_semaphore()
+    for k in range(1, n):
+        pl.semaphore_signal(
+            barrier,
+            inc=1,
+            device_id={axis: lax.rem(me + k, n)},
+            device_id_type=pl.DeviceIdType.MESH,
+        )
+    pl.semaphore_wait(barrier, n - 1)
+
+
+def exchange_kernel(axis, n, m, *refs):
+    sources, slots = refs[:m], refs[m : 2 * m]
+    send_sem, recv_sem = refs[2 * m :]
+    me = lax.axis_index(axis)
+    greet(axis, n, me)
+    copies = []
+    for k in range(1, n):
+        target = lax.rem(me + k, n)
+        for i in range(m):
+            copies.append(
+                pltpu.make_async_remote_copy(
+                    src_ref=sources[i].at[target],
+                    dst_ref=slots[i].at[k - 1],
+                    send_sem=send_sem.at[i, k - 1],
+                    recv_sem=recv_sem.at[i, k - 1],
+                    device_id={axis: target},
+                    device_id_type=pl.DeviceIdType.MESH,
+                )
+            )
+            copies[-1].start()
+    for copy in copies:
+        copy.wait()
+
+
+def sum_scatter(arrays, axis, collective_id):
+    n = lax.axis_size(axis)
+    me = lax.axis_index(axis)
+    m = len(arrays)
+    blocked = [a.reshape(n, a.shape[0] // n, a.shape[1]) for a in arrays]
+    sent = sum((n - 1) * b[0].size * b.dtype.itemsize for b in blocked)
+    received = pl.pallas_call(
+        functools.partial(exchange_kernel, axis, n, m),
+        out_shape=[jax.ShapeDtypeStruct((n - 1,) + b.shape[1:], b.dtype) for b in blocked],
+        in_specs=[pl.BlockSpec(memory_space=pl.ANY)] * m,
+        out_specs=[pl.BlockSpec(memory_space=pl.ANY)] * m,
+        scratch_shapes=[
+            pltpu.SemaphoreType.DMA((m, n - 1)),
+            pltpu.SemaphoreType.DMA((m, n - 1)),
+        ],
+        cost_estimate=pl.CostEstimate(flops=0, bytes_accessed=20 * sent, transcendentals=0),
+        compiler_params=pltpu.CompilerParams(collective_id=collective_id, has_side_effects=True),
+    )(*blocked)
+    totals = []
+    for b, r in zip(blocked, received):
+        own = lax.dynamic_index_in_dim(b, me, 0, keepdims=False).astype(jnp.float32)
+        totals.append(own + jnp.sum(r.astype(jnp.float32), axis=0))
+    return totals
+
+
+def gather_kernel(axis, n, source, gathered, send_sem, recv_sem, own_sem):
+    me = lax.axis_index(axis)
+    greet(axis, n, me)
+    copies = []
+    for k in range(1, n):
+        copies.append(
+            pltpu.make_async_remote_copy(
+                src_ref=source,
+                dst_ref=gathered.at[me],
+                send_sem=send_sem.at[k - 1],
+                recv_sem=recv_sem.at[k - 1],
+                device_id={axis: lax.rem(me + k, n)},
+                device_id_type=pl.DeviceIdType.MESH,
+            )
+        )
+        copies[-1].start()
+    own = pltpu.make_async_copy(source, gathered.at[me], own_sem)
+    own.start()
+    own.wait()
+    for copy in copies:
+        copy.wait()
+
+
+def gather_rows(array, axis, collective_id):
+    n = lax.axis_size(axis)
+    sent = (n - 1) * array.size * array.dtype.itemsize
+    gathered = pl.pallas_call(
+        functools.partial(gather_kernel, axis, n),
+        out_shape=jax.ShapeDtypeStruct((n,) + array.shape, array.dtype),
+        in_specs=[pl.BlockSpec(memory_space=pltpu.VMEM)],
+        out_specs=pl.BlockSpec(memory_space=pl.ANY),
+        scratch_shapes=[
+            pltpu.SemaphoreType.DMA((n - 1,)),
+            pltpu.SemaphoreType.DMA((n - 1,)),
+            pltpu.SemaphoreType.DMA,
+        ],
+        cost_estimate=pl.CostEstimate(flops=0, bytes_accessed=20 * sent, transcendentals=0),
+        compiler_params=pltpu.CompilerParams(collective_id=collective_id, has_side_effects=True),
+    )(array)
+    return gathered.reshape(n * array.shape[0], array.shape[1])
+
+
+def relay_kernel(axis, n, source, gathered, send_sem, recv_sem, side_send, side_recv, own_sem):
+    m = n // 2
+    reach = m // 2
+    half = source.shape[0] // 2
+    me = lax.axis_index(axis)
+    z, x = me // 2, lax.rem(me, 2)
+    partner = z * 2 + 1 - x
+    sides = (lax.rem(z + 1, m) * 2 + x, lax.rem(z + m - 1, m) * 2 + x)
+    barrier = pltpu.get_barrier_semaphore()
+    for device in (partner,) + sides:
+        pl.semaphore_signal(
+            barrier, inc=1, device_id={axis: device}, device_id_type=pl.DeviceIdType.MESH
+        )
+    pl.semaphore_wait(barrier, 3)
+
+    def hop(way, c, h):
+        back = h - 1 if way == 0 else m - h + 1
+        slot = lax.rem(z + m - back, m) * 2 + (x if c == 0 else 1 - x)
+        src = source if h == 1 and c == 0 else gathered.at[slot]
+        dst = gathered.at[slot]
+        if h == reach:
+            rows = pl.ds(way * half, half)
+            src, dst = src.at[rows], dst.at[rows]
+        return pltpu.make_async_remote_copy(
+            src_ref=src,
+            dst_ref=dst,
+            send_sem=send_sem.at[way, c, h - 1],
+            recv_sem=recv_sem.at[way, c, h - 1],
+            device_id={axis: sides[way]},
+            device_id_type=pl.DeviceIdType.MESH,
+        )
+
+    hops = {(w, c, h): hop(w, c, h) for w in (0, 1) for c in (0, 1) for h in range(1, reach + 1)}
+    across = pltpu.make_async_remote_copy(
+        src_ref=source,
+        dst_ref=gathered.at[me],
+        send_sem=side_send,
+        recv_sem=side_recv,
+        device_id={axis: partner},
+        device_id_type=pl.DeviceIdType.MESH,
+    )
+    across.start()
+    for w in (0, 1):
+        hops[w, 0, 1].start()
+    own = pltpu.make_async_copy(source, gathered.at[me], own_sem)
+    own.start()
+    across.wait_recv()
+    for w in (0, 1):
+        hops[w, 1, 1].start()
+    for h in range(1, reach + 1):
+        for c in (0, 1):
+            for w in (0, 1):
+                hops[w, c, h].wait_recv()
+                if h < reach:
+                    hops[w, c, h + 1].start()
+    own.wait()
+    across.wait_send()
+    for copy in hops.values():
+        copy.wait_send()
+
+
+def relay_rows(array, axis, collective_id):
+    n = lax.axis_size(axis)
+    if n % 4 or n < 8:
+        return gather_rows(array, axis, collective_id)
+    sent = (n - 1) * array.size * array.dtype.itemsize
+    ways = (2, 2, n // 4)
+    gathered = pl.pallas_call(
+        functools.partial(relay_kernel, axis, n),
+        out_shape=jax.ShapeDtypeStruct((n,) + array.shape, array.dtype),
+        in_specs=[pl.BlockSpec(memory_space=pltpu.VMEM)],
+        out_specs=pl.BlockSpec(memory_space=pl.ANY),
+        scratch_shapes=[
+            pltpu.SemaphoreType.DMA(ways),
+            pltpu.SemaphoreType.DMA(ways),
+            pltpu.SemaphoreType.DMA,
+            pltpu.SemaphoreType.DMA,
+            pltpu.SemaphoreType.DMA,
+        ],
+        cost_estimate=pl.CostEstimate(flops=0, bytes_accessed=20 * sent, transcendentals=0),
+        compiler_params=pltpu.CompilerParams(collective_id=collective_id, has_side_effects=True),
+    )(array)
+    return gathered.reshape(n * array.shape[0], array.shape[1])
+
+
+def spread(column):
+    return jnp.broadcast_to(column[:, None], (column.shape[0], 128))
 
 
 def per_device(
@@ -94,57 +290,42 @@
     scaled = (wide_in * attn_gain.astype(jnp.float32)).astype(jnp.bfloat16)
     squares = jnp.sum(wide_in * wide_in, axis=1)
     partial_sum = jnp.dot(scaled, qkv_weight, preferred_element_type=jnp.float32)
-    own_proj, own_squares = (
-        lax.psum_scatter(partial_sum, "gx", scatter_dimension=0, tiled=True),
-        lax.psum_scatter(squares, "gx", scatter_dimension=0, tiled=True),
+    own_proj, own_squares = sum_scatter(
+        [partial_sum.astype(jnp.bfloat16), spread(squares)], "gx", 0
     )
     own_lengths = lax.dynamic_slice_in_dim(lengths, row_start, local_rows, 0)
     query_rows, fresh_key_rows, new_values = make_heads(
-        own_proj, own_squares, own_lengths, groups, per_kv
+        own_proj, own_squares[:, 0], own_lengths, groups, per_kv
     )
     attn = attend(query_rows, fresh_key_rows, new_values, cache_keys, cache_values, own_lengths)
     attn = attn.reshape(local_rows, groups * per_kv * HD)
     proj_part = jnp.dot(
-        lax.all_gather(attn, "gx", axis=0, tiled=True),
-        out_weight,
-        preferred_element_type=jnp.float32,
-    )
-    attn_proj = lax.psum(proj_part, "gy")
-    alive_col = live_mask.astype(jnp.float32)[:, None]
-    residual = (wide_in + alive_col * attn_proj).astype(jnp.bfloat16)
-    resid_wide = residual.astype(jnp.float32)
+        relay_rows(attn, "gx", 1), out_weight, preferred_element_type=jnp.float32
+    )
+    out_rows = batch_size // lax.axis_size("gy")
+    out_start = lax.axis_index("gy") * out_rows
+    (attn_proj,) = sum_scatter([proj_part.astype(jnp.bfloat16)], "gy", 2)
+    alive_rows = lax.dynamic_slice_in_dim(live_mask, out_start, out_rows, 0)
+    alive_rows = alive_rows.astype(jnp.float32)[:, None]
+    token_rows = lax.dynamic_slice_in_dim(tokens, out_start, out_rows, 0).astype(jnp.float32)
+    resid_rows = (token_rows + alive_rows * attn_proj).astype(jnp.bfloat16)
+    resid_wide = gather_rows(resid_rows, "gy", 3).astype(jnp.float32)
     mlp_in = (resid_wide * mlp_gain.astype(jnp.float32)).astype(jnp.bfloat16)
     resid_squares = jnp.sum(resid_wide * resid_wide, axis=1)
-    out_rows = batch_size // lax.axis_size("gy")
-    out_start = lax.axis_index("gy") * out_rows
-    square_all = lax.psum(resid_squares, "gx")
-    hidden_width = gate_weight.shape[1]
-    stacked = lax.psum_scatter(
-        jnp.concatenate(
-            (
-                jnp.dot(mlp_in, gate_weight, preferred_element_type=jnp.float32),
-                jnp.dot(mlp_in, up_weight, preferred_element_type=jnp.float32),
-            ),
-            axis=1,
-        ),
+    gate_part = jnp.dot(mlp_in, gate_weight, preferred_element_type=jnp.float32)
+    up_part = jnp.dot(mlp_in, up_weight, preferred_element_type=jnp.float32)
+    gate_sum, up_sum, own_all = sum_scatter(
+        [gate_part.astype(jnp.bfloat16), up_part.astype(jnp.bfloat16), spread(resid_squares)],
         "gx",
-        scatter_dimension=0,
-        tiled=True,
-    )
-    own_all = lax.dynamic_slice_in_dim(square_all, row_start, local_rows, 0)
-    mlp_scale = lax.rsqrt(own_all / D + NORM_EPS)[:, None]
-    hidden_share = (
-        jax.nn.silu(stacked[:, :hidden_width] * mlp_scale) * (stacked[:, hidden_width:] * mlp_scale)
-    ).astype(jnp.bfloat16)
+        4,
+    )
+    mlp_scale = lax.rsqrt(own_all[:, :1] / D + NORM_EPS)
+    hidden_share = (jax.nn.silu(gate_sum * mlp_scale) * (up_sum * mlp_scale)).astype(jnp.bfloat16)
     down_full = jnp.dot(
-        lax.all_gather(hidden_share, "gx", axis=0, tiled=True),
-        down_weight,
-        preferred_element_type=jnp.float32,
-    )
-    down_sum = lax.psum_scatter(down_full, "gy", scatter_dimension=0, tiled=True)
-    resid_rows = lax.dynamic_slice_in_dim(resid_wide, out_start, out_rows, 0)
-    alive_rows = lax.dynamic_slice_in_dim(alive_col, out_start, out_rows, 0)
-    return (resid_rows + alive_rows * down_sum).astype(jnp.bfloat16)
+        relay_rows(hidden_share, "gx", 5), down_weight, preferred_element_type=jnp.float32
+    )
+    (down_sum,) = sum_scatter([down_full.astype(jnp.bfloat16)], "gy", 6)
+    return (resid_rows.astype(jnp.float32) + alive_rows * down_sum).astype(jnp.bfloat16)
 
 
 def solution(mesh):

time: 551 us -> 392 us (0.71)
  waiting for transfers between devices: 428 us -> 0 us
  Pallas kernels: 0 us -> 313 us
  blocking collectives: 45.5 us -> 0 us
  between operations: 14.3 us -> 0.28 us
  other arithmetic: 14.6 us -> 21.3 us
  matrix products: 47 us -> 53.2 us
    pallas_call x0 -> x7, Pallas kernels: none -> 313 us  [the longest x4 170 us: sum_scatter(): pl.pallas_call(functools.partial(exchange_kernel, axis, n, m), out_shape=...]
    reduce_scatter x3 -> x0, waiting for transfers between devices: 288 us -> none  [the longest x1 215 us: per_device(): lax.psum_scatter(jnp.concatenate((jnp.dot(mlp_in, gate_weight, preferred_...]
    all_gather x2 -> x0, waiting for transfers between devices: 105 us -> none  [the longest x1 65.2 us: per_device(): lax.all_gather(hidden_share, 'gx', axis=0, tiled=True)]
    psum x1 -> x0, waiting for transfers between devices: 35.1 us -> none  [per_device(): attn_proj = lax.psum(proj_part, 'gy')]
    unnamed x1 -> x0, blocking collectives: 23.5 us -> none
    psum x1 -> x0, blocking collectives: 22 us -> none  [per_device(): square_all = lax.psum(resid_squares, 'gx')]
    reduce_sum x0 -> x6, other arithmetic: none -> 9.62 us  [sum_scatter(): totals.append(own + jnp.sum(r.astype(jnp.float32), axis=0))]
    dot_general x4, matrix products: 30.5 us -> 37.1 us  [the longest x1 11.1 us: per_device(): jnp.dot(relay_rows(hidden_share, 'gx', 5), down_weight, preferred_element...]
  transfers between devices with their start and end apart: 6 -> 0, of which waited for: 6 -> 0; matrix products, arithmetic and copies ran while one was open for 0% -> 0% of each run, Pallas kernels for 0% -> 0%
where the time goes in v1:
time: 392 us; the launch traced here: 390 us
  Pallas kernels  313 us (80%)
  matrix products  53.2 us (14%)
  other arithmetic  21.3 us (5%)
    pallas_call x4, Pallas kernels, sum_scatter(): pl.pallas_call(functools.partial(exchange_kernel, axis, n, m), out_shape=...  170 us
    pallas_call x2, Pallas kernels, relay_rows(): pl.pallas_call(functools.partial(relay_kernel, axis, n), out_shape=jax.Sh...  134 us
    dot_general x1, matrix products, per_device(): jnp.dot(relay_rows(hidden_share, 'gx', 5), down_weight, preferred_element...  11.1 us
    dot_general x1, matrix products, per_device(): gate_part = jnp.dot(mlp_in, gate_weight, preferred_element_type=jnp.float32)  10.8 us
    dot_general x1, matrix products, per_device(): up_part = jnp.dot(mlp_in, up_weight, preferred_element_type=jnp.float32)  10.7 us
    reduce_sum x6, other arithmetic, sum_scatter(): totals.append(own + jnp.sum(r.astype(jnp.float32), axis=0))  9.62 us
    pallas_call x1, Pallas kernels, gather_rows(): pl.pallas_call(functools.partial(gather_kernel, axis, n), out_shape=jax.S...  9 us

profile of v1, /device:TPU:0, one launch (start us, length us, event | category | flops | bytes accessed | tf_op | source)
XLA Modules:
  0.0 390.2 jit_solution(9950435433321105025)
XLA Ops:
  0.0 1.2 fusion.4
  2.0 5.2 %convolution_convert_fusion.2 = bf16[256,2560]{1,0:T(8,128)(2,1)} fusion(bf16[1024,2560]{1,0:T(8,128)(2,1)} %param.14, bf16[256,1024]{1,0:T(8,128)(2,1)} %param.12, f32[1024]{0:T(1024)S(1)} %convert_element_type.140), kind=kOutput, calls=%fused_computation.4 | convolution fusion | flops 1343619072 | bytes 7081984 | tf_op jit(solution)/shard_map/dot_general | solution.py:292
  8.0 29.6 %shard_map.118 = (bf16[7,32,2560]{2,1,0:T(8,128)(2,1)}, f32[7,32,128]{2,1,0:T(8,128)}) custom-call(bf16[8,32,2560]{2,1,0:T(8,128)(2,1)} %bitcast.60, f32[8,32,128]{2,1,0:T(8,128)} %broadcast_in_dim.28.refs_1_), custom_call_target="tpu_custom_call" | custom-call | bytes 25231360 | tf_op jit(solution)/shard_map/pallas_call | solution.py:120
  38.7 0.9 dynamic-slice_convert_fusion
  39.8 1.4 convert_reduce_fusion.2
  42.5 5.8 %fusion.40 = (f32[32,2,8]{2,1,0:T(2,128)S(1)}, f32[32,2,8,512]{3,2,1,0:T(8,128)S(1)}) fusion(bf16[32,2,512,128]{3,2,1,0:T(8,128)(2,1)} %param.15, bf16[32,2,8,64]{3,2,1,0:T(8,128)(2,1)S(1)} %get-tuple-element.20, bf16[32,2,8,64]{3,2,1,0:T(8,128)(2,1)S(1)} %get-tuple-element.19, pred[32,512]{1,0:T(8,128)(4,1)S(1)} %iota_compare_fusion), kind=kOutput, calls=%fused_computation.82 | convolution fusion | flops 68156928 | bytes 9586688 | tf_op jit(solution)/shard_map/bgqd,bgld->bgql/dot_general | solution.py:52
  48.8 4.7 %fusion.2 = bf16[32,2,8,128]{3,2,1,0:T(8,128)(2,1)S(1)} fusion(bf16[32,2,512,128]{3,2,1,0:T(8,128)(2,1)} %param.16, f32[32,2,8]{2,1,0:T(2,128)S(1)} %get-tuple-element.15, f32[32,2,128]{2,1,0:T(2,128)S(1)} %bitcast.72, f32[32,2,8]{2,1,0:T(2,128)S(1)} %get-tuple-element.16, f32[32,2,8,512]{3,2,1,0:T(8,128)S(1)} %get-tuple-element.26, ...), kind=kOutput, calls=%fused_computation.14 | convolution fusion | flops 68157440 | bytes 9623552 | tf_op jit(solution)/shard_map/bgql,bgld->bgqd/dot_general | solution.py:67
  54.2 29.7 %shard_map.119 = bf16[8,32,2048]{2,1,0:T(8,128)(2,1)} custom-call(bf16[32,2048]{1,0:T(8,128)(2,1)} %bitcast.67), custom_call_target="tpu_custom_call" | custom-call | bytes 18350080 | tf_op jit(solution)/shard_map/pallas_call | solution.py:248
  84.0 4.6 %convolution_convert_fusion.4 = bf16[256,1024]{1,0:T(8,128)(2,1)} fusion(bf16[256,2048]{1,0:T(8,128)(2,1)} %bitcast.62, bf16[2048,1024]{1,0:T(8,128)(2,1)} %param.19), kind=kOutput, calls=%fused_computation.11 | convolution fusion | flops 1074003968 | bytes 5767168 | tf_op jit(solution)/shard_map/dot_general | solution.py:302
  88.6 8.0 %shard_map.120 = bf16[3,64,1024]{2,1,0:T(8,128)(2,1)} custom-call(bf16[4,64,1024]{2,1,0:T(8,128)(2,1)} %bitcast.65), custom_call_target="tpu_custom_call" | custom-call | bytes 7864320 | tf_op jit(solution)/shard_map/pallas_call | solution.py:120
  96.6 1.1 convert_reduce_fusion.5
  97.8 1.7 fusion.17.source
  99.5 9.0 %shard_map.121 = bf16[4,64,1024]{2,1,0:T(8,128)(2,1)} custom-call(bf16[64,1024]{1,0:T(8,128)(2,1)} %fusion.17.source), custom_call_target="tpu_custom_call" | custom-call | bytes 7864320 | tf_op jit(solution)/shard_map/pallas_call | solution.py:165
  108.5 1.1 fusion.5
  109.7 10.8 %convolution_convert_fusion.1 = bf16[256,7168]{1,0:T(8,128)(2,1)} fusion(bf16[256,1024]{1,0:T(8,128)(2,1)S(1)} %fusion.5, bf16[1024,7168]{1,0:T(8,128)(2,1)} %param.21), kind=kOutput, calls=%fused_computation.1 | convolution fusion | flops 3759931392 | bytes 18874368 | tf_op jit(solution)/shard_map/dot_general | solution.py:315
  120.5 10.7 %convolution_convert_fusion = bf16[256,7168]{1,0:T(8,128)(2,1)} fusion(bf16[256,1024]{1,0:T(8,128)(2,1)S(1)} %fusion.5, bf16[1024,7168]{1,0:T(8,128)(2,1)} %param.22), kind=kOutput, calls=%fused_computation | convolution fusion | flops 3759931392 | bytes 18874368 | tf_op jit(solution)/shard_map/dot_general | solution.py:316
  132.2 125.6 %shard_map.122 = (bf16[7,32,7168]{2,1,0:T(8,128)(2,1)}, bf16[7,32,7168]{2,1,0:T(8,128)(2,1)}, f32[7,32,128]{2,1,0:T(8,128)}) custom-call(bf16[8,32,7168]{2,1,0:T(8,128)(2,1)} %bitcast.55, bf16[8,32,7168]{2,1,0:T(8,128)(2,1)} %bitcast.57, f32[8,32,128]{2,1,0:T(8,128)} %broadcast_in_dim.32.refs_2_), custom_call_target="tpu_custom_call" | custom-call | bytes 130744320 | tf_op jit(solution)/shard_map/pallas_call | solution.py:120
  258.9 4.2 %convert_reduce_fusion = (f32[32,7168]{1,0:T(8,128)S(1)}, f32[32,7168]{1,0:T(8,128)S(1)}) fusion(bf16[7,32,7168]{2,1,0:T(8,128)(2,1)} %get-tuple-element.14, bf16[7,32,7168]{2,1,0:T(8,128)(2,1)} %get-tuple-element.12), kind=kLoop, calls=%fused_computation.2 | loop fusion | flops 5963776 | bytes 8257536 | tf_op jit(solution)/shard_map/reduce_sum | solution.py:135
  263.1 2.3 fusion.8.source
  265.4 104.1 %shard_map.123 = bf16[8,32,7168]{2,1,0:T(8,128)(2,1)} custom-call(bf16[32,7168]{1,0:T(8,128)(2,1)} %fusion.8.source), custom_call_target="tpu_custom_call" | custom-call | bytes 64225280 | tf_op jit(solution)/shard_map/pallas_call | solution.py:248
  369.5 11.1 %convolution_convert_fusion.3 = bf16[256,1024]{1,0:T(8,128)(2,1)} fusion(bf16[256,7168]{1,0:T(8,128)(2,1)} %bitcast.59, bf16[7168,1024]{1,0:T(8,128)(2,1)} %param.23), kind=kOutput, calls=%fused_computation.10 | convolution fusion | flops 3758358528 | bytes 18874368 | tf_op jit(solution)/shard_map/dot_general | solution.py:324
  380.6 6.9 %shard_map.124 = bf16[3,64,1024]{2,1,0:T(8,128)(2,1)} custom-call(bf16[4,64,1024]{2,1,0:T(8,128)(2,1)} %bitcast.63), custom_call_target="tpu_custom_call" | custom-call | bytes 7864320 | tf_op jit(solution)/shard_map/pallas_call | solution.py:120
  387.5 1.1 convert_reduce_fusion.4
  388.5 1.7 fusion.14
  (42 shorter events, 7.3 us)
Async XLA Ops:
  7.2 34.2 %copy-start.3 = (s32[256]{0:T(256)S(1)}, s32[256]{0:T(256)}, u32[]{:S(2)}) copy-start(s32[256]{0:T(256)} %param.17) | copy-start | bytes 3076
  53.5 44.2 %copy-start.4 = (s32[256]{0:T(256)S(1)}, s32[256]{0:T(256)}, u32[]{:S(2)}) copy-start(s32[256]{0:T(256)} %param.18) | copy-start | bytes 3076
  84.0 24.5 %copy-start.2 = (bf16[1024]{0:T(1024)(128)(2,1)S(1)}, bf16[1024]{0:T(1024)(128)(2,1)}, u32[]{:S(2)}) copy-start(bf16[1024]{0:T(1024)(128)(2,1)} %param.20) | copy-start | bytes 6148
  120.5 10.7 %copy-start = (bf16[4,64,1024]{2,1,0:T(8,128)(2,1)S(1)}, bf16[4,64,1024]{2,1,0:T(8,128)(2,1)}, u32[]{:S(2)}) copy-start(bf16[4,64,1024]{2,1,0:T(8,128)(2,1)} %shard_map.121) | copy-start | bytes 1572868
  369.5 19.1 %copy-start.1 = (bf16[64,1024]{1,0:T(8,128)(2,1)S(1)}, bf16[64,1024]{1,0:T(8,128)(2,1)}, u32[]{:S(2)}) copy-start(bf16[64,1024]{1,0:T(8,128)(2,1)} %fusion.17.source) | copy-start | bytes 393220
